TPU v7x, 32 devices: a whole 2x2x4 slice. The times are simulated.
32 devices in a mesh: dp: 2 (over core), expert: 4 (over y, x), mp: 4 (over z).
Axes of the slice: x: 2, y: 2, z: 4, core: 2. Of those that a mesh axis runs over, the one named last changes fastest.
Arguments:
- hidden: bfloat16 [3072, 2, 7168], P(('dp', 'expert'), None, 'mp'), may hold values from -6 to 6
- cotangent: bfloat16 [3072, 2048], P(('dp', 'expert'), 'mp'), may hold values from -6 to 6
- routes: int32 [3072, 2], P(('dp', 'expert')), may hold values from 0 to 3, all different within a row; in each aligned block of 384 rows (0 to 383, 384 to 767, ...) at most 288 rows name the same one
- combine: float32 [3072, 2], P(('dp', 'expert')), may hold values from 0.1 to 0.9
- block_pair: int32 [8, 12], P(('dp', 'expert')), may hold values from 0 to 11, each once within a row
- lengths: int32 [8, 12], P(('dp', 'expert')), may hold values from 4 to 32
- log_ratio: float32 [8, 12], P(('dp', 'expert')), may hold values from -30 to 30
Outputs:
- grad_down: float32 [4, 7168, 2048], P('expert', ('mp', 'dp'))
- expert_load: float32 [4], replicated
Inputs may be any that keep to these rules, and one draw needn't show every extreme that they name: `routes`: each row names 2 different experts; in each aligned block of 384 rows (the rows of one device) no expert is named more than 288 times, and in some blocks one expert is named exactly 288 times. `block_pair`: each row holds every number of 0 to 11 once; value v marks the chosen response of the row's pair v // 2 if v is even, its rejected response if v is odd.
All inputs are finite; a program needn't handle non-finite values.
Results may differ from a plain program's by a relative error of at most 0.0029.
Values may be sent and summed in bfloat16 or wider, within the bound.
No kernel may reach another device: no remote copies, remote signals or barrier semaphores. Data moves between devices by JAX's collectives and lax.ppermute only.
A program may use at most 128 MiB of HBM per device.

v0:
```python
import jax
import jax.numpy as jnp
from jax import lax
from jax.sharding import PartitionSpec as P

EXP_DEV = 1
LEN = 32
beta_scale = 0.1


def token_weights(combine, block_pair, lengths, log_ratio, block_len):
    blocks = block_pair.shape[1]
    labels = jnp.arange(blocks, dtype=jnp.int32)
    matches = block_pair[:, :, None] == labels[None, None, :]
    by_label = jnp.sum(jnp.where(matches, log_ratio[:, :, None], 0.0), axis=1)
    margin = by_label[:, 0::2] - by_label[:, 1::2]
    pair_coef = beta_scale * jax.nn.sigmoid(-beta_scale * margin)
    owners = block_pair // 2
    pair_ids = jnp.arange(blocks // 2, dtype=jnp.int32)
    picked = owners[:, :, None] == pair_ids[None, None, :]
    block_coef = jnp.sum(jnp.where(picked, pair_coef[:, None, :], 0.0), axis=2)
    block_weight = jnp.where(block_pair % 2 == 0, -block_coef, block_coef)
    position = jnp.arange(block_len, dtype=jnp.int32)
    within = position[None, None, :] < lengths[:, :, None]
    per_token = jnp.where(within, block_weight[:, :, None], 0.0).reshape(-1)
    return (combine * per_token[:, None], within.reshape(-1))


def body(hidden, cotangent, routes, combine, block_pair, lengths, log_ratio):
    weight, within = token_weights(combine, block_pair, lengths, log_ratio, LEN)
    tok_rows = routes.shape[0]
    route_top = routes.shape[1]
    ff_local = hidden.shape[2]
    groups = lax.axis_size("expert")
    experts = groups * EXP_DEV
    most_rows = 3 * tok_rows // 4
    labels = jnp.arange(experts, dtype=jnp.int32)
    routed = routes[:, :, None] == labels[None, None, :]
    local_load = jnp.sum(jnp.where(routed & within[:, None, None], 1.0, 0.0), axis=(0, 1)).astype(
        jnp.float32
    )
    flat_rows = tok_rows * route_top
    flat_hits = routed.reshape(flat_rows, experts).astype(jnp.int32)
    rank_of = jnp.sum((jnp.cumsum(flat_hits, axis=0) - 1) * flat_hits, axis=1)
    slot_of = routes.reshape(flat_rows) * most_rows + rank_of
    source = (
        jnp.zeros((experts * most_rows,), jnp.int32)
        .at[slot_of]
        .set(jnp.arange(flat_rows, dtype=jnp.int32))
    )
    filled = jnp.zeros((experts * most_rows,), jnp.float32).at[slot_of].set(1.0)
    token_of = source // route_top
    slot_weight = jnp.take(weight.reshape(flat_rows), source) * filled
    packed_h = jnp.take(hidden.reshape(flat_rows, ff_local), source, axis=0).reshape(
        groups, EXP_DEV * most_rows, ff_local
    )
    narrow_s = (
        slot_weight[:, None] * jnp.take(cotangent, token_of, axis=0).astype(jnp.float32)
    ).astype(jnp.bfloat16)
    moved_h, narrow = (
        lax.all_to_all(packed_h, "expert", split_axis=0, concat_axis=0, tiled=True),
        lax.all_to_all(
            narrow_s.reshape(groups, EXP_DEV * most_rows, cotangent.shape[1]),
            "expert",
            split_axis=0,
            concat_axis=0,
            tiled=True,
        ),
    )
    moved_s = lax.all_gather(narrow, "mp", axis=2, tiled=True)
    moved_h = moved_h.reshape(groups, EXP_DEV, most_rows, ff_local)
    moved_s = moved_s.reshape(groups, EXP_DEV, most_rows, moved_s.shape[2])
    products = [
        lax.dot_general(
            moved_h[:, 0],
            moved_s[:, 0],
            (((0, 1), (0, 1)), ((), ())),
            preferred_element_type=jnp.float32,
        )
    ]
    owned = lax.psum_scatter(jnp.stack(products, axis=1), "dp", scatter_dimension=0, tiled=True)
    grad_down = jnp.transpose(owned, (1, 0, 2))
    expert_load = lax.psum(local_load, ("dp", "expert"))
    return (grad_down, expert_load)


def solution(mesh):
    in_specs = (
        P(("dp", "expert"), None, "mp"),
        P(("dp", "expert"), "mp"),
        P(("dp", "expert"), None),
        P(("dp", "expert"), None),
        P(("dp", "expert"), None),
        P(("dp", "expert"), None),
        P(("dp", "expert"), None),
    )
    out_specs = (P("expert", ("mp", "dp"), None), P())
    return jax.shard_map(body, mesh=mesh, in_specs=in_specs, out_specs=out_specs, check_vma=False)
```

profile of v0, /device:TPU:0, one launch (start us, length us, event | category | flops | bytes accessed | tf_op | source)
XLA Modules:
  0.0 187.8 jit_solution(6503914561430639834)
XLA Ops:
  7.2 0.8 fusion.6
  8.2 0.7 fusion.14
  8.9 0.7 broadcast_multiply_fusion.1
  9.6 0.8 copy.16
  11.0 1.1 reduce-window.6
  12.2 0.2 slice_reduce_fusion
  12.7 3.4 %scatter_custom_fusion = s32[1152]{0:T(1024)S(1)} fusion(s32[768]{0:T(1024)S(1)} %fusion.11, s32[768]{0:T(1024)S(1)} %iota.36, s32[]{:T(128)} %constant.86.clone.1), kind=kCustom, calls=%fused_computation.39 | custom fusion | bytes 4612 | tf_op jit(solution)/shard_map/scatter | solution.py:49
  16.3 0.7 fusion.13
  17.1 0.7 broadcast_reduce_fusion.1
  18.0 0.7 broadcast_multiply_fusion
  19.0 3.4 %scatter_custom_fusion.1 = f32[1152]{0:T(1024)S(1)} fusion(s32[768]{0:T(1024)S(1)} %fusion.11, f32[768]{0:T(1024)S(1)} %broadcast.245, f32[]{:T(128)} %constant.96.clone.1), kind=kCustom, calls=%fused_computation.37 | custom fusion | bytes 4612 | tf_op jit(solution)/shard_map/scatter | solution.py:51
  22.4 4.6 %gather_fusion.1 = f32[1152]{0:T(1024)S(1)} fusion(f32[768]{0:T(1024)S(1)} %reshape.294, s32[2048]{0:T(1024)S(1)} %pad_clamp_fusion.1), kind=kCustom, calls=%fused_computation.1 | custom fusion | bytes 13824 | tf_op jit(solution)/shard_map/jit(_take)/gather | solution.py:53
  27.2 4.2 %gather_fusion.2 = bf16[1152,512]{1,0:T(8,128)(2,1)S(1)} fusion(bf16[384,512]{1,0:T(8,128)(2,1)S(1)} %copy-done, s32[2048]{0:T(1024)S(1)} %pad_clamp_fusion), kind=kCustom, calls=%fused_computation.2 | custom fusion | bytes 2363904 | tf_op jit(solution)/shard_map/jit(_take)/gather | solution.py:58
  31.5 0.4 multiply_convert_fusion
  31.8 20.6 %all_to_all.10 = bf16[4,288,512]{2,1,0:T(8,128)(2,1)} all-to-all(bf16[4,288,512]{2,1,0:T(8,128)(2,1)S(1)} %multiply_convert_fusion), channel_id=1, replica_groups=mesh['dp'=2,'expert'=4,'mp'=4] {'expert'}, dimensions={0} | all-to-all | bytes 2359296 | tf_op jit(solution)/shard_map/all_to_all | solution.py:62
  52.6 5.7 %reshape.293 = bf16[768,1792]{1,0:T(8,128)(2,1)S(1)} reshape(bf16[384,2,1792]{2,1,0:T(2,128)(2,1)} %param.7) | data formatting | bytes 5505024 | tf_op jit(solution)/shard_map/reshape | solution.py:54
  58.4 5.6 %gather_fusion = bf16[1152,1792]{1,0:T(8,128)(2,1)} fusion(bf16[768,1792]{1,0:T(8,128)(2,1)S(1)} %reshape.293, s32[2048]{0:T(1024)S(1)} %pad_clamp_fusion.1), kind=kCustom, calls=%fused_computation | custom fusion | bytes 8262144 | tf_op jit(solution)/shard_map/jit(_take)/gather | solution.py:54
  64.0 2.6 %broadcast_select_fusion = bf16[4,288,1792]{2,1,0:T(8,128)(2,1)S(1)} fusion(bf16[4,288,1792]{2,1,0:T(8,128)(2,1)} %bitcast.39, pred[4,288]{1,0:T(4,128)(4,1)S(1)} %broadcast_in_dim.106), kind=kLoop, calls=%fused_computation.6 | loop fusion | flops 2064384 | bytes 8258688 | tf_op jit(solution)/shard_map/jit(_take)/select_n | solution.py:54
  66.6 49.7 %all_to_all.11 = bf16[4,288,1792]{2,1,0:T(8,128)(2,1)} all-to-all(bf16[4,288,1792]{2,1,0:T(8,128)(2,1)S(1)} %broadcast_select_fusion), channel_id=1, replica_groups=mesh['dp'=2,'expert'=4,'mp'=4] {'expert'}, dimensions={0} | all-to-all | bytes 8257536 | tf_op jit(solution)/shard_map/all_to_all | solution.py:61
  116.4 25.4 %all-gather.2.cloned.1.call-done = bf16[4,288,2048]{2,1,0:T(8,128)(2,1)} async-done(((bf16[4,288,512]{2,1,0:T(8,128)(2,1)}), bf16[4,288,2048]{2,1,0:T(8,128)(2,1)}) %all-gather.2.cloned.1.call-update) | async-done | bytes 4718608 | tf_op jit(solution)/shard_map/all_gather | solution.py:70
  141.8 15.8 %convolution_bitcast_fusion = f32[1792,1,2048]{2,0,1:T(8,128)} fusion(bf16[4,288,1792]{2,1,0:T(8,128)(2,1)} %all_to_all.11, bf16[4,288,2048]{2,1,0:T(8,128)(2,1)} %all-gather.2.cloned.1.call-done), kind=kOutput, calls=%fused_computation.5 | convolution fusion | flops 8455716864 | bytes 23527424 | tf_op jit(solution)/shard_map/dot_general | solution.py:74
  157.6 0.7 copy-done.1
  158.3 14.8 %psum.7 = f32[4]{0:T(128)} all-reduce(f32[4]{0:T(128)S(1)} %select_reduce_fusion), channel_id=1, replica_groups=mesh['dp'=2,'expert'=4,'mp'=4] {'dp','expert'}, use_global_device_ids=true, to_apply=%region_9.10 | all-reduce | flops 4 | bytes 32 | tf_op jit(solution)/shard_map/psum | solution.py:83
  173.1 7.8 %reduce-scatter.2.cloned.1.call-done = f32[896,1,2048]{2,0,1:T(8,128)} async-done(((f32[1792,1,2048]{2,0,1:T(8,128)}), f32[896,1,2048]{2,0,1:T(8,128)}) %reduce-scatter.2.cloned.1.call-update) | async-done | bytes 7340048 | tf_op jit(solution)/shard_map/reduce_scatter | solution.py:81
  (39 shorter events, 2.4 us)
Async XLA Ops:
  7.2 20.0 %copy-start = (bf16[384,512]{1,0:T(8,128)(2,1)S(1)}, bf16[384,512]{1,0:T(8,128)(2,1)}, u32[]{:S(2)}) copy-start(bf16[384,512]{1,0:T(8,128)(2,1)} %param.8) | copy-start | bytes 1179652
  7.2 134.6 %all-gather.2.cloned.1.call-start = ((), (), s32[]{:S(2)}) async-start(), calls=%async_computation.3 | async-start | bytes 5898240 | tf_op jit(solution)/shard_map/all_gather | solution.py:70
  52.5 128.4 %reduce-scatter.2.cloned.1.call-start = ((), (), s32[]{:S(2)}) async-start(), calls=%async_computation.4 | async-start | bytes 22020096 | tf_op jit(solution)/shard_map/reduce_scatter | solution.py:81
  157.5 0.7 copy-start.1
Sparse Core Ops, SparseCore 0:
  52.6 89.0 all-gather.1
  157.7 23.2 reduce-scatter.1
where the time goes:
time: 188 us
  blocking collectives  85.2 us (45%)
  waiting for transfers between devices  33.3 us (18%)
  local copies, waits for them, and re-layouts  31 us (16%)
  matrix products  15.8 us (8%)
  between operations  14.3 us (8%)
  other arithmetic  8.25 us (4%)
    all_to_all x1, blocking collectives, body(): lax.all_to_all(packed_h, 'expert', split_axis=0, concat_axis=0, tiled=True)  49.7 us
    all_gather x1, waiting for transfers between devices, body(): moved_s = lax.all_gather(narrow, 'mp', axis=2, tiled=True)  25.4 us
    all_to_all x1, blocking collectives, body(): lax.all_to_all(narrow_s.reshape(groups, EXP_DEV * most_rows, cotangent.sh...  20.6 us
    dot_general x1, matrix products, body(): lax.dot_general(moved_h[:, 0], moved_s[:, 0], (((0, 1), (0, 1)), ((), ())...  15.8 us
    psum x1, blocking collectives, body(): expert_load = lax.psum(local_load, ('dp', 'expert'))  14.8 us
    reduce_scatter x1, waiting for transfers between devices, body(): lax.psum_scatter(jnp.stack(products, axis=1), 'dp', scatter_dimension=0,...  7.84 us
    reshape x1, local copies, waits for them, and re-layouts, body(): hidden.reshape(flat_rows, ff_local)  5.71 us
    gather x1, local copies, waits for them, and re-layouts, body(): jnp.take(hidden.reshape(flat_rows, ff_local), source, axis=0)  5.63 us
  transfers between devices with their start and end apart: 2, of which 2 were waited for; matrix products, arithmetic and copies ran while one was open for 8% of the time, Pallas kernels for 0%

commit v1 on v0

--- a/solution.py
+++ b/solution.py
@@ -6,6 +6,16 @@
 EXP_DEV = 1
 LEN = 32
 beta_scale = 0.1
+
+
+def gather_by_hops(x, name, d):
+    size = lax.axis_size(name)
+    moving, parts = (x, [x])
+    for _ in range(size - 1):
+        moving = lax.ppermute(moving, name, [(i, (i + 1) % size) for i in range(size)])
+        parts.insert(0, moving)
+    line = jnp.concatenate(parts, axis=d)
+    return jnp.roll(line, (lax.axis_index(name) + 1) * x.shape[d], axis=d)
 
 
 def token_weights(combine, block_pair, lengths, log_ratio, block_len):
@@ -67,7 +77,7 @@
             tiled=True,
         ),
     )
-    moved_s = lax.all_gather(narrow, "mp", axis=2, tiled=True)
+    moved_s = gather_by_hops(narrow, "mp", 2)
     moved_h = moved_h.reshape(groups, EXP_DEV, most_rows, ff_local)
     moved_s = moved_s.reshape(groups, EXP_DEV, most_rows, moved_s.shape[2])
     products = [

time: 188 us -> 195 us (1.037)
  blocking collectives: 85.2 us -> 35.9 us
  waiting for transfers between devices: 33.3 us -> 66.4 us
  local copies, waits for them, and re-layouts: 31 us -> 45.6 us
  starting transfers between devices: 0.08 us -> 6.45 us
    ppermute x0 -> x3, waiting for transfers between devices: none -> 59.7 us  [gather_by_hops(): lax.ppermute(moving, name, [(i, (i + 1) % size) for i in range(size)])]
    all_to_all x1 -> x0, blocking collectives: 49.7 us -> none  [body(): lax.all_to_all(packed_h, 'expert', split_axis=0, concat_axis=0, tiled=True)]
    all_gather x1 -> x0, waiting for transfers between devices: 25.4 us -> none  [body(): moved_s = lax.all_gather(narrow, 'mp', axis=2, tiled=True)]
    unnamed x5 -> x12, local copies, waits for them, and re-layouts: 1.48 us -> 13.6 us
    all_to_all x0 -> x1, starting transfers between devices: none -> 4.83 us  [body(): lax.all_to_all(packed_h, 'expert', split_axis=0, concat_axis=0, tiled=True)]
    concatenate x0 -> x1, local copies, waits for them, and re-layouts: none -> 2.52 us  [gather_by_hops(): return jnp.roll(line, (lax.axis_index(name) + 1) * x.shape[d], axis=d)]
    select_n x2, other arithmetic: 2.61 us -> 4.61 us  [body(): jnp.take(hidden.reshape(flat_rows, ff_local), source, axis=0)]
  transfers between devices with their start and end apart: 2 -> 5, of which waited for: 2 -> 4; matrix products, arithmetic and copies ran while one was open for 8% -> 16% of each run, Pallas kernels for 0% -> 0%
where the time goes in v1:
time: 195 us
  waiting for transfers between devices  66.4 us (34%)
  local copies, waits for them, and re-layouts  45.6 us (23%)
  blocking collectives  35.9 us (18%)
  matrix products  15.8 us (8%)
  between operations  14.2 us (7%)
  other arithmetic  10.2 us (5%)
  starting transfers between devices  6.45 us (3%)
    ppermute x3, waiting for transfers between devices, gather_by_hops(): lax.ppermute(moving, name, [(i, (i + 1) % size) for i in range(size)])  59.7 us
    all_to_all x1, blocking collectives, body(): lax.all_to_all(narrow_s.reshape(groups, EXP_DEV * most_rows, cotangent.sh...  20.6 us
    dot_general x1, matrix products, body(): lax.dot_general(moved_h[:, 0], moved_s[:, 0], (((0, 1), (0, 1)), ((), ())...  15.8 us
    psum x1, blocking collectives, body(): expert_load = lax.psum(local_load, ('dp', 'expert'))  15.3 us
    unnamed x12, local copies, waits for them, and re-layouts  13.6 us
    reduce_scatter x1, waiting for transfers between devices, body(): lax.psum_scatter(jnp.stack(products, axis=1), 'dp', scatter_dimension=0,...  6.68 us
    reshape x1, local copies, waits for them, and re-layouts, body(): hidden.reshape(flat_rows, ff_local)  5.71 us
    gather x1, local copies, waits for them, and re-layouts, body(): jnp.take(hidden.reshape(flat_rows, ff_local), source, axis=0)  5.63 us
  transfers between devices with their start and end apart: 5, of which 4 were waited for; matrix products, arithmetic and copies ran while one was open for 16% of the time, Pallas kernels for 0%

profile of v1, /device:TPU:0, one launch (start us, length us, event | category | flops | bytes accessed | tf_op | source)
XLA Modules:
  0.0 194.6 jit_solution(9840566931638105291)
XLA Ops:
  12.7 3.4 %scatter_custom_fusion = s32[1152]{0:T(1024)S(1)} fusion(s32[768]{0:T(1024)S(1)} %fusion.12, s32[768]{0:T(1024)S(1)} %iota.36, s32[]{:T(128)} %constant.109.clone.1), kind=kCustom, calls=%fused_computation.48 | custom fusion | bytes 4612 | tf_op jit(solution)/shard_map/scatter | solution.py:59
  19.1 3.4 %scatter_custom_fusion.1 = f32[1152]{0:T(1024)S(1)} fusion(s32[768]{0:T(1024)S(1)} %fusion.12, f32[768]{0:T(1024)S(1)} %broadcast.246, f32[]{:T(128)} %constant.119.clone.1), kind=kCustom, calls=%fused_computation.46 | custom fusion | bytes 4612 | tf_op jit(solution)/shard_map/scatter | solution.py:61
  22.5 4.6 %gather_fusion.1 = f32[1152]{0:T(1024)S(1)} fusion(f32[768]{0:T(1024)S(1)} %reshape.294, s32[2048]{0:T(1024)S(1)} %get-tuple-element.9), kind=kCustom, calls=%fused_computation.1 | custom fusion | bytes 13824 | tf_op jit(solution)/shard_map/jit(_take)/gather | solution.py:63
  27.1 4.2 %gather_fusion.2 = bf16[1152,512]{1,0:T(8,128)(2,1)S(1)} fusion(bf16[384,512]{1,0:T(8,128)(2,1)S(1)} %copy-done, s32[2048]{0:T(1024)S(1)} %get-tuple-element.8), kind=kCustom, calls=%fused_computation.2 | custom fusion | bytes 2363904 | tf_op jit(solution)/shard_map/jit(_take)/gather | solution.py:68
  31.8 20.6 %all_to_all.10 = bf16[4,288,512]{2,1,0:T(8,128)(2,1)} all-to-all(bf16[4,288,512]{2,1,0:T(8,128)(2,1)S(1)} %multiply_convert_fusion), channel_id=1, replica_groups=mesh['dp'=2,'expert'=4,'mp'=4] {'expert'}, dimensions={0} | all-to-all | bytes 2359296 | tf_op jit(solution)/shard_map/all_to_all | solution.py:72
  52.4 1.6 collective-permute-start
  54.1 5.7 %reshape.293 = bf16[768,1792]{1,0:T(8,128)(2,1)S(1)} reshape(bf16[384,2,1792]{2,1,0:T(2,128)(2,1)} %param.7) | data formatting | bytes 5505024 | tf_op jit(solution)/shard_map/reshape | solution.py:64
  59.8 5.6 %gather_fusion = bf16[1152,1792]{1,0:T(8,128)(2,1)} fusion(bf16[768,1792]{1,0:T(8,128)(2,1)S(1)} %reshape.293, s32[2048]{0:T(1024)S(1)} %get-tuple-element.9), kind=kCustom, calls=%fused_computation | custom fusion | bytes 8262144 | tf_op jit(solution)/shard_map/jit(_take)/gather | solution.py:64
  65.4 15.4 %collective-permute-done = bf16[4,288,512]{2,1,0:T(8,128)(2,1)} collective-permute-done((bf16[4,288,512]{2,1,0:T(8,128)(2,1)}, bf16[4,288,512]{2,1,0:T(8,128)(2,1)}, u32[]{:S(2)}, u32[]{:S(2)}) %collective-permute-start) | collective-permute-done | bytes 1179680 | tf_op jit(solution)/shard_map/ppermute | solution.py:15
  80.8 4.6 %broadcast_select_fusion = bf16[4,288,1792]{2,1,0:T(8,128)(2,1)} fusion(bf16[4,288,1792]{2,1,0:T(8,128)(2,1)} %bitcast.38, pred[4,288]{1,0:T(4,128)(4,1)S(1)} %broadcast_in_dim.106), kind=kLoop, calls=%fused_computation.7 | loop fusion | flops 2064384 | bytes 8258688 | tf_op jit(solution)/shard_map/jit(_take)/select_n | solution.py:64
  85.4 4.8 %all-to-all-start = ((bf16[4,288,1792]{2,1,0:T(8,128)(2,1)}), bf16[4,288,1792]{2,1,0:T(8,128)(2,1)}, u32[]{:S(2)}, u32[]{:S(2)}) async-start(bf16[4,288,1792]{2,1,0:T(8,128)(2,1)} %broadcast_select_fusion), calls=%async_computation | async-start | bytes 8257536 | tf_op jit(solution)/shard_map/all_to_all | solution.py:71
  90.3 17.9 %collective-permute-done.1 = bf16[4,288,512]{2,1,0:T(8,128)(2,1)S(1)} collective-permute-done((bf16[4,288,512]{2,1,0:T(8,128)(2,1)}, bf16[4,288,512]{2,1,0:T(8,128)(2,1)S(1)}, u32[]{:S(2)}, u32[]{:S(2)}) %collective-permute-start.1) | collective-permute-done | bytes 1179680 | tf_op jit(solution)/shard_map/ppermute | solution.py:15
  108.2 26.4 %collective-permute-done.2 = bf16[4,288,512]{2,1,0:T(8,128)(2,1)S(1)} collective-permute-done((bf16[4,288,512]{2,1,0:T(8,128)(2,1)S(1)}, bf16[4,288,512]{2,1,0:T(8,128)(2,1)S(1)}, u32[]{:S(2)}, u32[]{:S(2)}) %collective-permute-start.2) | collective-permute-done | bytes 1179680 | tf_op jit(solution)/shard_map/ppermute | solution.py:15
  134.6 1.2 constant_dynamic-update-slice_fusion.7
  135.8 1.2 constant_dynamic-update-slice_fusion.6
  137.0 2.5 %constant_dynamic-update-slice_fusion.5 = bf16[4,288,4096]{2,1,0:T(8,128)(2,1)} fusion(bf16[4,288,4096]{2,1,0:T(8,128)(2,1)} %constant_dynamic-update-slice_fusion.6, bf16[4,288,512]{2,1,0:T(8,128)(2,1)} %collective-permute-done), kind=kLoop, calls=%fused_computation.18 | loop fusion | bytes 2359296
  139.5 2.5 %constant_dynamic-update-slice_fusion.4 = bf16[4,288,4096]{2,1,0:T(8,128)(2,1)} fusion(bf16[4,288,4096]{2,1,0:T(8,128)(2,1)} %constant_dynamic-update-slice_fusion.5, bf16[4,288,512]{2,1,0:T(8,128)(2,1)} %all_to_all.10), kind=kLoop, calls=%fused_computation.17 | loop fusion | bytes 2359296
  141.9 1.2 constant_dynamic-update-slice_fusion.3
  143.1 1.2 constant_dynamic-update-slice_fusion.2
  144.3 2.4 %constant_dynamic-update-slice_fusion.1 = bf16[4,288,4096]{2,1,0:T(8,128)(2,1)} fusion(bf16[4,288,4096]{2,1,0:T(8,128)(2,1)} %constant_dynamic-update-slice_fusion.2, bf16[4,288,512]{2,1,0:T(8,128)(2,1)} %collective-permute-done), kind=kLoop, calls=%fused_computation.14 | loop fusion | bytes 2359296
  146.7 2.5 %constant_dynamic-update-slice_fusion = bf16[4,288,4096]{2,1,0:T(8,128)(2,1)} fusion(bf16[4,288,4096]{2,1,0:T(8,128)(2,1)} %constant_dynamic-update-slice_fusion.1, bf16[4,288,512]{2,1,0:T(8,128)(2,1)} %all_to_all.10), kind=kLoop, calls=%fused_computation.13 | loop fusion | bytes 2359296 | tf_op jit(solution)/shard_map/jit(_roll_dynamic)/concatenate | solution.py:18
  149.2 15.8 %convolution_bitcast_fusion = f32[1792,1,2048]{2,0,1:T(8,128)} fusion(bf16[4,288,1792]{2,1,0:T(8,128)(2,1)} %all-to-all-done, bf16[4,288,4096]{2,1,0:T(8,128)(2,1)} %constant_dynamic-update-slice_fusion, s32[]{:T(128)S(6)} %select_n.126), kind=kOutput, calls=%fused_computation.5 | convolution fusion | flops 8455716864 | bytes 23527428 | tf_op jit(solution)/shard_map/dot_general | solution.py:84
  165.8 15.3 %psum.7 = f32[4]{0:T(128)} all-reduce(f32[4]{0:T(128)S(1)} %select_reduce_fusion), channel_id=1, replica_groups=mesh['dp'=2,'expert'=4,'mp'=4] {'dp','expert'}, use_global_device_ids=true, to_apply=%region_9.10 | all-reduce | flops 4 | bytes 32 | tf_op jit(solution)/shard_map/psum | solution.py:93
  181.1 6.7 %reduce-scatter.2.cloned.1.call-done = f32[896,1,2048]{2,0,1:T(8,128)} async-done(((f32[1792,1,2048]{2,0,1:T(8,128)}), f32[896,1,2048]{2,0,1:T(8,128)}) %reduce-scatter.2.cloned.1.call-update) | async-done | bytes 7340048 | tf_op jit(solution)/shard_map/reduce_scatter | solution.py:91
  (50 shorter events, 9.8 us)
Async XLA Ops:
  7.2 20.0 %copy-start = (bf16[384,512]{1,0:T(8,128)(2,1)S(1)}, bf16[384,512]{1,0:T(8,128)(2,1)}, u32[]{:S(2)}) copy-start(bf16[384,512]{1,0:T(8,128)(2,1)} %param.8) | copy-start | bytes 1179652
  52.4 28.4 %collective-permute-start = (bf16[4,288,512]{2,1,0:T(8,128)(2,1)}, bf16[4,288,512]{2,1,0:T(8,128)(2,1)}, u32[]{:S(2)}, u32[]{:S(2)}) collective-permute-start(bf16[4,288,512]{2,1,0:T(8,128)(2,1)} %all_to_all.10), channel_id=1, source_target_pairs={{0,1},{1,2},{2,3},{3,0},{4,5},{5,6},{6,7},{7,4},{8,9},{9,10},{10,1... | collective-permute-start | bytes 3538952 | tf_op jit(solution)/shard_map/ppermute | solution.py:15
  80.8 27.4 %collective-permute-start.1 = (bf16[4,288,512]{2,1,0:T(8,128)(2,1)}, bf16[4,288,512]{2,1,0:T(8,128)(2,1)S(1)}, u32[]{:S(2)}, u32[]{:S(2)}) collective-permute-start(bf16[4,288,512]{2,1,0:T(8,128)(2,1)} %collective-permute-done), channel_id=1, source_target_pairs={{0,1},{1,2},{2,3},{3,0},{4,5},{5,6},{6,7},{7,4},{8,9},{9,10},{10,1... | collective-permute-start | bytes 3538952 | tf_op jit(solution)/shard_map/ppermute | solution.py:15
  85.4 63.8 %all-to-all-start = ((bf16[4,288,1792]{2,1,0:T(8,128)(2,1)}), bf16[4,288,1792]{2,1,0:T(8,128)(2,1)}, u32[]{:S(2)}, u32[]{:S(2)}) async-start(bf16[4,288,1792]{2,1,0:T(8,128)(2,1)} %broadcast_select_fusion), calls=%async_computation | async-start | bytes 8257536 | tf_op jit(solution)/shard_map/all_to_all | solution.py:71
  90.2 97.5 %reduce-scatter.2.cloned.1.call-start = ((), (), s32[]{:S(2)}) async-start(), calls=%async_computation.3 | async-start | bytes 22020096 | tf_op jit(solution)/shard_map/reduce_scatter | solution.py:91
  108.2 26.4 %collective-permute-start.2 = (bf16[4,288,512]{2,1,0:T(8,128)(2,1)S(1)}, bf16[4,288,512]{2,1,0:T(8,128)(2,1)S(1)}, u32[]{:S(2)}, u32[]{:S(2)}) collective-permute-start(bf16[4,288,512]{2,1,0:T(8,128)(2,1)S(1)} %collective-permute-done.1), channel_id=1, source_target_pairs={{0,1},{1,2},{2,3},{3,0},{4,5},{5,6},{6,7},{7,4},{8,9},{9,10},{10,1... | collective-permute-start | bytes 3538952 | tf_op jit(solution)/shard_map/ppermute | solution.py:15
  165.0 0.7 copy-start.1
Sparse Core Ops, SparseCore 0:
  165.2 22.5 reduce-scatter.1
